TPU v7x, 32 devices: a whole 2x2x4 slice. The times are simulated.
32 devices in a mesh: sx: 4 (over x, core), sy: 2 (over y), px: 4 (over z).
Axes of the slice: x: 2, y: 2, z: 4, core: 2. Of those that a mesh axis runs over, the one named last changes fastest.
Arguments:
- patterns: bfloat16 [64, 64, 9216], P('sx', 'sy', 'px'), may hold values from -6 to 6
- basis: bfloat16 [9216, 256], P('px', ('sx', 'sy')), may hold values from -0.375 to 0.375
- valid: int32 [64, 64], P('sx', 'sy'), may hold values 0 or 1
- strength: float32 [64, 64], P('sx', 'sy'), may hold values from 0.25 to 2
Outputs:
- denoised: bfloat16 [64, 64, 9216], P('sx', 'sy', 'px')
Inputs may be any that keep to these rules, and one draw needn't show every extreme that they name: `valid`: 1 marks an on-sample scan position, 0 an off-sample one.
All inputs are finite; a program needn't handle non-finite values. No bound on the sum of `valid` on one device may be relied on, other than what follows from the above.
Results may differ from a plain program's by a relative error of at most 0.0089.
Values may be sent and summed in bfloat16 or wider, within the bound.
No kernel may reach another device: no remote copies, remote signals or barrier semaphores. Data moves between devices by JAX's collectives and lax.ppermute only.
A program may use at most 64 MiB of HBM per device.

v0:
```python
import jax
import jax.numpy as jnp
from jax import lax
from jax.sharding import PartitionSpec as P

PIX = 9216
RADIUS = 3


def extended(array, sides, width):
    for axis, dim in sides:
        count, length = (lax.axis_size(axis), array.shape[dim])
        up = [(i, (i + 1) % count) for i in range(count - 1)]
        down = [(j, i) for i, j in up]
        last = lax.slice_in_dim(array, length - width, length, axis=dim)
        initial = lax.slice_in_dim(array, 0, width, axis=dim)
        before = lax.ppermute(last, axis, up)
        after = lax.ppermute(initial, axis, down)
        array = jnp.concatenate([before, array, after], axis=dim)
    return array


def neighbour_steps():
    steps = []
    for row_step in range(-RADIUS, RADIUS + 1):
        for col_step in range(-RADIUS, RADIUS + 1):
            if row_step != 0 or col_step != 0:
                steps.append((row_step, col_step))
    return steps


def squared_gaps(center, padded):
    rows, cols = (center.shape[0], center.shape[1])
    gaps = []
    for row_step, col_step in neighbour_steps():
        other = padded[
            RADIUS + row_step : RADIUS + row_step + rows,
            RADIUS + col_step : RADIUS + col_step + cols,
        ]
        differ = center - other
        gaps.append(jnp.sum(differ * differ, axis=-1))
    return jnp.stack(gaps)


def blend(center, padded, mask_pad, gaps, strength):
    rows, cols = (center.shape[0], center.shape[1])
    factor = 1.0 / (2.0 * PIX * strength)
    numerator = center
    total = jnp.ones((rows, cols), jnp.float32)
    for index, (row_step, col_step) in enumerate(neighbour_steps()):
        other = padded[
            RADIUS + row_step : RADIUS + row_step + rows,
            RADIUS + col_step : RADIUS + col_step + cols,
        ]
        mask_other = mask_pad[
            RADIUS + row_step : RADIUS + row_step + rows,
            RADIUS + col_step : RADIUS + col_step + cols,
        ]
        weight = mask_other * jnp.exp(-gaps[index] * factor)
        numerator = numerator + weight[:, :, None] * other
        total = total + weight
    return numerator / total[:, :, None]


def extend(coeffs, mask_full):
    return (
        extended(coeffs, (("sx", 0), ("sy", 1)), RADIUS),
        extended(mask_full, (("sx", 0), ("sy", 1)), RADIUS),
    )


def on_device(patterns, basis, valid, strength):
    cells_x, cells_y, pixels = patterns.shape
    flat = patterns.reshape(cells_x * cells_y, pixels)
    whole_basis = lax.all_gather(basis, ("sx", "sy"), axis=1, tiled=True)
    partial_value = jnp.dot(flat, whole_basis, preferred_element_type=jnp.float32)
    partial_value = partial_value.reshape(cells_x, cells_y, partial_value.shape[1])
    mask_full = valid.astype(jnp.float32)
    coeffs = lax.psum(partial_value, "px")
    padded, mask_pad = extend(coeffs, mask_full)
    gaps = squared_gaps(coeffs, padded)
    average = blend(coeffs, padded, mask_pad, gaps, strength).astype(jnp.bfloat16)
    avg_flat = average.reshape(cells_x * cells_y, average.shape[2])
    rebuilt = lax.dot_general(
        avg_flat, whole_basis, (((1,), (1,)), ((), ())), preferred_element_type=jnp.float32
    )
    return rebuilt.astype(jnp.bfloat16).reshape(cells_x, cells_y, pixels)


def solution(mesh):
    return jax.shard_map(
        on_device,
        mesh=mesh,
        in_specs=(P("sx", "sy", "px"), P("px", ("sx", "sy")), P("sx", "sy"), P("sx", "sy")),
        out_specs=P("sx", "sy", "px"),
        check_vma=False,
    )
```

profile of v0, /device:TPU:1, one launch (start us, length us, event | category | flops | bytes accessed | tf_op | source)
XLA Modules:
  0.0 117.6 jit_solution(7627593339896749223)
XLA Ops:
  6.5 0.0 copy-start
  6.5 0.0 all-gather.2.cloned.1.call-start
  6.5 0.7 all-gather.2.cloned.1.call-update
  7.3 0.0 copy-start.4
  7.3 0.0 all-reduce.2.cloned.1.call-start
  7.3 28.3 %all-gather.2.cloned.1.call-done = bf16[2304,256]{0,1:T(8,128)(2,1)} async-done(((bf16[2304,32]{0,1:T(8,128)(2,1)}), bf16[2304,256]{0,1:T(8,128)(2,1)}) %all-gather.2.cloned.1.call-update) | async-done | bytes 1179664 | tf_op jit(solution)/shard_map/all_gather | solution.py:75
  35.6 0.0 copy-done
  35.6 2.9 %fusion = f32[16,32,256]{2,1,0:T(8,128)} fusion(bf16[16,32,2304]{2,1,0:T(8,128)(2,1)S(1)} %copy-done, bf16[2304,256]{0,1:T(8,128)(2,1)} %all-gather.2.cloned.1.call-done), kind=kOutput, calls=%fused_computation.81 | convolution fusion | flops 603979776 | bytes 4063232 | tf_op jit(solution)/shard_map/dot_general | solution.py:76
  38.5 0.0 all-reduce.2.cloned.1.call-update
  38.5 0.0 copy-done.4
  38.6 3.3 %collective-permute-start = (f32[3,32]{1,0:T(4,128)S(1)}, f32[3,32]{1,0:T(4,128)S(1)}, u32[]{:S(2)}, u32[]{:S(2)}) collective-permute-start(f32[3,32]{1,0:T(4,128)S(1)} %get-tuple-element.124), channel_id=1, source_target_pairs={{0,8},{8,16},{16,24},{1,9},{9,17},{17,25},{2,10},{10,18},{18,26},{... | collective-permute-start | bytes 1160 | tf_op jit(solution)/shard_map/ppermute | solution.py:17
  41.8 1.9 %collective-permute-start.1 = (f32[3,32]{1,0:T(4,128)S(1)}, f32[3,32]{1,0:T(4,128)S(1)}, u32[]{:S(2)}, u32[]{:S(2)}) collective-permute-start(f32[3,32]{1,0:T(4,128)S(1)} %get-tuple-element.125), channel_id=1, source_target_pairs={{8,0},{16,8},{24,16},{9,1},{17,9},{25,17},{10,2},{18,10},{26,18},{... | collective-permute-start | bytes 1160 | tf_op jit(solution)/shard_map/ppermute | solution.py:18
  43.8 0.0 collective-permute-done
  43.8 3.4 %collective-permute-done.1 = f32[3,32]{1,0:T(4,128)S(1)} collective-permute-done((f32[3,32]{1,0:T(4,128)S(1)}, f32[3,32]{1,0:T(4,128)S(1)}, u32[]{:S(2)}, u32[]{:S(2)}) %collective-permute-start.1) | collective-permute-done | bytes 416 | tf_op jit(solution)/shard_map/ppermute | solution.py:18
  47.1 28.8 %all-reduce.2.cloned.1.call-done = f32[16,32,256]{2,1,0:T(8,128)} async-done(((f32[16,32,256]{2,1,0:T(8,128)}), f32[16,32,256]{2,1,0:T(8,128)}) %all-reduce.2.cloned.1.call-update) | async-done | bytes 524304 | tf_op jit(solution)/shard_map/psum | solution.py:79
  76.0 0.0 copy-start.1
  76.0 1.0 fusion.59
  77.0 4.6 %collective-permute-start.3 = (f32[3,32,256]{2,1,0:T(8,128)S(1)}, f32[3,32,256]{2,1,0:T(8,128)S(1)}, u32[]{:S(2)}, u32[]{:S(2)}) collective-permute-start(f32[3,32,256]{2,1,0:T(8,128)S(1)} %get-tuple-element.116), channel_id=1, source_target_pairs={{0,8},{8,16},{16,24},{1,9},{9,17},{17,25},{2,10},{10,18},{18,26},{... | collective-permute-start | bytes 294920 | tf_op jit(solution)/shard_map/ppermute | solution.py:17
  81.6 0.1 fusion.60
  81.7 3.1 %collective-permute-start.2 = (f32[22,3]{1,0:T(8,128)S(1)}, f32[22,3]{1,0:T(8,128)S(1)}, u32[]{:S(2)}, u32[]{:S(2)}) collective-permute-start(f32[22,3]{1,0:T(8,128)S(1)} %get-tuple-element.123), channel_id=1, source_target_pairs={{0,4},{1,5},{2,6},{3,7},{8,12},{9,13},{10,14},{11,15},{16,20},{17,... | collective-permute-start | bytes 800 | tf_op jit(solution)/shard_map/ppermute | solution.py:17
  84.7 1.3 %collective-permute-start.6 = (f32[22,3]{1,0:T(8,128)S(1)}, f32[22,3]{1,0:T(8,128)S(1)}, u32[]{:S(2)}, u32[]{:S(2)}) collective-permute-start(f32[22,3]{1,0:T(8,128)S(1)} %get-tuple-element.122), channel_id=1, source_target_pairs={{4,0},{5,1},{6,2},{7,3},{12,8},{13,9},{14,10},{15,11},{20,16},{21,... | collective-permute-start | bytes 800 | tf_op jit(solution)/shard_map/ppermute | solution.py:18
  86.0 1.9 %collective-permute-start.4 = (f32[3,32,256]{2,1,0:T(8,128)S(1)}, f32[3,32,256]{2,1,0:T(8,128)S(1)}, u32[]{:S(2)}, u32[]{:S(2)}) collective-permute-start(f32[3,32,256]{2,1,0:T(8,128)S(1)} %get-tuple-element.117), channel_id=1, source_target_pairs={{8,0},{16,8},{24,16},{9,1},{17,9},{25,17},{10,2},{18,10},{26,18},{... | collective-permute-start | bytes 294920 | tf_op jit(solution)/shard_map/ppermute | solution.py:18
  88.0 0.0 collective-permute-done.3
  88.0 1.2 constant_dynamic-update-slice_fusion.1
  89.2 2.8 %collective-permute-done.4 = f32[3,32,256]{2,1,0:T(8,128)S(1)} collective-permute-done((f32[3,32,256]{2,1,0:T(8,128)S(1)}, f32[3,32,256]{2,1,0:T(8,128)S(1)}, u32[]{:S(2)}, u32[]{:S(2)}) %collective-permute-start.4) | collective-permute-done | bytes 98336 | tf_op jit(solution)/shard_map/ppermute | solution.py:18
  92.0 1.3 %collective-permute-start.7 = (f32[22,3,256]{2,1,0:T(4,128)S(1)}, f32[22,3,256]{2,1,0:T(4,128)S(1)}, u32[]{:S(2)}, u32[]{:S(2)}) collective-permute-start(f32[22,3,256]{2,1,0:T(4,128)S(1)} %get-tuple-element.111), channel_id=1, source_target_pairs={{4,0},{5,1},{6,2},{7,3},{12,8},{13,9},{14,10},{15,11},{20,16},{21,... | collective-permute-start | bytes 202760 | tf_op jit(solution)/shard_map/ppermute | solution.py:18
  93.3 0.0 collective-permute-done.2
  93.3 0.0 collective-permute-done.6
  93.4 0.1 pad_maximum_fusion.3
  93.4 4.0 %collective-permute-start.5 = (f32[22,3,256]{2,1,0:T(4,128)S(1)}, f32[22,3,256]{2,1,0:T(4,128)S(1)}, u32[]{:S(2)}, u32[]{:S(2)}) collective-permute-start(f32[22,3,256]{2,1,0:T(4,128)S(1)} %get-tuple-element.112), channel_id=1, source_target_pairs={{0,4},{1,5},{2,6},{3,7},{8,12},{9,13},{10,14},{11,15},{16,20},{17,... | collective-permute-start | bytes 202760 | tf_op jit(solution)/shard_map/ppermute | solution.py:17
  97.4 0.0 collective-permute-done.7
  97.4 0.0 copy-done.1
  97.4 1.0 multiply_reduce_fusion.42
  98.4 1.0 multiply_reduce_fusion.43
  99.4 0.0 collective-permute-done.5
  99.4 1.1 multiply_reduce_fusion.46
  100.6 1.1 multiply_reduce_fusion.47
  101.7 0.0 copy-start.3
  101.7 1.2 %multiply_reduce_fusion.45 = (f32[16,32]{1,0:T(8,128)S(1)}, f32[16,32]{1,0:T(8,128)S(1)}, f32[16,32]{1,0:T(8,128)S(1)}, f32[16,32]{1,0:T(8,128)S(1)}, f32[16,32]...) fusion(f32[16,32,256]{2,1,0:T(8,128)S(1)} %copy-done.1, ...), kind=kLoop, calls=%fused_computation.171 | loop fusion | flops 5498880 | bytes 4550656 | tf_op jit(solution)/shard_map/reduce_sum | solution.py:41
  102.9 0.0 copy-done.3
  102.9 0.2 add_add_fusion
  103.1 0.0 copy-start.2
  103.1 5.4 %divide_convert_fusion = bf16[16,32,256]{2,1,0:T(8,128)(2,1)S(1)} fusion(f32[16,32,256]{2,1,0:T(8,128)S(1)} %copy-done.1, f32[19,32,256]{2,1,0:T(8,128)S(1)} %constant_dynamic-update-slice_fusion.5, f32[19,32,256]{2,1,0:T(8,128)S(1)} %get-tuple-element.115, f32[22,32,256]{2,1,0:T(8,128)S(1)} %constant_dynamic-update-slice_fusion, ...), kind=kLoop, calls=%fused_computation.125 | loop fusion | flops 18350080 | bytes 4888576 | tf_op jit(solution)/shard_map/convert_element_type | solution.py:82
  108.6 0.0 copy-done.2
  108.6 2.2 %convolution_convert_fusion = bf16[512,2304]{1,0:T(8,128)(2,1)} fusion(bf16[512,256]{1,0:T(8,128)(2,1)S(1)} %bitcast.8, bf16[2304,256]{0,1:T(8,128)(2,1)S(1)} %copy-done.2), kind=kOutput, calls=%fused_computation.40 | convolution fusion | flops 605159424 | bytes 3801088 | tf_op jit(solution)/shard_map/dot_general | solution.py:84
  (7 shorter events, 0.1 us)
Async XLA Ops:
  6.5 29.1 %copy-start = (bf16[16,32,2304]{2,1,0:T(8,128)(2,1)S(1)}, bf16[16,32,2304]{2,1,0:T(8,128)(2,1)}, u32[]{:S(2)}) copy-start(bf16[16,32,2304]{2,1,0:T(8,128)(2,1)} %param.4) | copy-start | bytes 7077892
  6.5 29.1 %all-gather.2.cloned.1.call-start = ((), (), s32[]{:S(2)}) async-start(), calls=%async_computation | async-start | bytes 1327104 | tf_op jit(solution)/shard_map/all_gather | solution.py:75
  7.3 31.3 %copy-start.4 = (s32[16,32]{1,0:T(8,128)S(1)}, s32[16,32]{1,0:T(8,128)}, u32[]{:S(2)}) copy-start(s32[16,32]{1,0:T(8,128)} %param.6) | copy-start | bytes 6148
  7.3 68.7 %all-reduce.2.cloned.1.call-start = ((), (), s32[]{:S(2)}) async-start(), calls=%async_computation.1 | async-start | bytes 1048576 | tf_op jit(solution)/shard_map/psum | solution.py:79
  38.6 5.2 %collective-permute-start = (f32[3,32]{1,0:T(4,128)S(1)}, f32[3,32]{1,0:T(4,128)S(1)}, u32[]{:S(2)}, u32[]{:S(2)}) collective-permute-start(f32[3,32]{1,0:T(4,128)S(1)} %get-tuple-element.124), channel_id=1, source_target_pairs={{0,8},{8,16},{16,24},{1,9},{9,17},{17,25},{2,10},{10,18},{18,26},{... | collective-permute-start | bytes 1160 | tf_op jit(solution)/shard_map/ppermute | solution.py:17
  41.8 5.3 %collective-permute-start.1 = (f32[3,32]{1,0:T(4,128)S(1)}, f32[3,32]{1,0:T(4,128)S(1)}, u32[]{:S(2)}, u32[]{:S(2)}) collective-permute-start(f32[3,32]{1,0:T(4,128)S(1)} %get-tuple-element.125), channel_id=1, source_target_pairs={{8,0},{16,8},{24,16},{9,1},{17,9},{25,17},{10,2},{18,10},{26,18},{... | collective-permute-start | bytes 1160 | tf_op jit(solution)/shard_map/ppermute | solution.py:18
  76.0 21.5 %copy-start.1 = (f32[16,32,256]{2,1,0:T(8,128)S(1)}, f32[16,32,256]{2,1,0:T(8,128)}, u32[]{:S(2)}) copy-start(f32[16,32,256]{2,1,0:T(8,128)} %all-reduce.2.cloned.1.call-done) | copy-start | bytes 1572868
  77.0 11.0 %collective-permute-start.3 = (f32[3,32,256]{2,1,0:T(8,128)S(1)}, f32[3,32,256]{2,1,0:T(8,128)S(1)}, u32[]{:S(2)}, u32[]{:S(2)}) collective-permute-start(f32[3,32,256]{2,1,0:T(8,128)S(1)} %get-tuple-element.116), channel_id=1, source_target_pairs={{0,8},{8,16},{16,24},{1,9},{9,17},{17,25},{2,10},{10,18},{18,26},{... | collective-permute-start | bytes 294920 | tf_op jit(solution)/shard_map/ppermute | solution.py:17
  81.7 11.7 %collective-permute-start.2 = (f32[22,3]{1,0:T(8,128)S(1)}, f32[22,3]{1,0:T(8,128)S(1)}, u32[]{:S(2)}, u32[]{:S(2)}) collective-permute-start(f32[22,3]{1,0:T(8,128)S(1)} %get-tuple-element.123), channel_id=1, source_target_pairs={{0,4},{1,5},{2,6},{3,7},{8,12},{9,13},{10,14},{11,15},{16,20},{17,... | collective-permute-start | bytes 800 | tf_op jit(solution)/shard_map/ppermute | solution.py:17
  84.7 8.6 %collective-permute-start.6 = (f32[22,3]{1,0:T(8,128)S(1)}, f32[22,3]{1,0:T(8,128)S(1)}, u32[]{:S(2)}, u32[]{:S(2)}) collective-permute-start(f32[22,3]{1,0:T(8,128)S(1)} %get-tuple-element.122), channel_id=1, source_target_pairs={{4,0},{5,1},{6,2},{7,3},{12,8},{13,9},{14,10},{15,11},{20,16},{21,... | collective-permute-start | bytes 800 | tf_op jit(solution)/shard_map/ppermute | solution.py:18
  86.0 5.9 %collective-permute-start.4 = (f32[3,32,256]{2,1,0:T(8,128)S(1)}, f32[3,32,256]{2,1,0:T(8,128)S(1)}, u32[]{:S(2)}, u32[]{:S(2)}) collective-permute-start(f32[3,32,256]{2,1,0:T(8,128)S(1)} %get-tuple-element.117), channel_id=1, source_target_pairs={{8,0},{16,8},{24,16},{9,1},{17,9},{25,17},{10,2},{18,10},{26,18},{... | collective-permute-start | bytes 294920 | tf_op jit(solution)/shard_map/ppermute | solution.py:18
  92.0 5.4 %collective-permute-start.7 = (f32[22,3,256]{2,1,0:T(4,128)S(1)}, f32[22,3,256]{2,1,0:T(4,128)S(1)}, u32[]{:S(2)}, u32[]{:S(2)}) collective-permute-start(f32[22,3,256]{2,1,0:T(4,128)S(1)} %get-tuple-element.111), channel_id=1, source_target_pairs={{4,0},{5,1},{6,2},{7,3},{12,8},{13,9},{14,10},{15,11},{20,16},{21,... | collective-permute-start | bytes 202760 | tf_op jit(solution)/shard_map/ppermute | solution.py:18
  93.4 6.0 %collective-permute-start.5 = (f32[22,3,256]{2,1,0:T(4,128)S(1)}, f32[22,3,256]{2,1,0:T(4,128)S(1)}, u32[]{:S(2)}, u32[]{:S(2)}) collective-permute-start(f32[22,3,256]{2,1,0:T(4,128)S(1)} %get-tuple-element.112), channel_id=1, source_target_pairs={{0,4},{1,5},{2,6},{3,7},{8,12},{9,13},{10,14},{11,15},{16,20},{17,... | collective-permute-start | bytes 202760 | tf_op jit(solution)/shard_map/ppermute | solution.py:17
  101.7 1.2 %copy-start.3 = (f32[16,32]{1,0:T(8,128)S(1)}, f32[16,32]{1,0:T(8,128)}, u32[]{:S(2)}) copy-start(f32[16,32]{1,0:T(8,128)} %param.7) | copy-start | bytes 6148
  103.1 5.5 %copy-start.2 = (bf16[2304,256]{0,1:T(8,128)(2,1)S(1)}, bf16[2304,256]{0,1:T(8,128)(2,1)}, u32[]{:S(2)}) copy-start(bf16[2304,256]{0,1:T(8,128)(2,1)} %all-gather.2.cloned.1.call-done) | copy-start | bytes 3538948
Sparse Core Ops, SparseCore 0:
  9.2 26.3 all-gather.1
  38.6 37.2 all-reduce.1
where the time goes:
time: 118 us
  waiting for transfers between devices  64.1 us (54%)
  starting transfers between devices  21.4 us (18%)
  between operations  13.7 us (12%)
  other arithmetic  11.1 us (9%)
  matrix products  5.06 us (4%)
  local copies, waits for them, and re-layouts  2.33 us (2%)
    psum x1, waiting for transfers between devices, on_device(): coeffs = lax.psum(partial_value, 'px')  28.8 us
    all_gather x1, waiting for transfers between devices, on_device(): whole_basis = lax.all_gather(basis, ('sx', 'sy'), axis=1, tiled=True)  28.3 us
    ppermute x4, starting transfers between devices, extended(): before = lax.ppermute(last, axis, up)  14.9 us
    ppermute x4, starting transfers between devices, extended(): after = lax.ppermute(initial, axis, down)  6.43 us
    ppermute x4, waiting for transfers between devices, extended(): after = lax.ppermute(initial, axis, down)  6.18 us
    convert_element_type x1, other arithmetic, on_device(): blend(coeffs, padded, mask_pad, gaps, strength).astype(jnp.bfloat16)  5.44 us
    reduce_sum x5, other arithmetic, squared_gaps(): gaps.append(jnp.sum(differ * differ, axis=-1))  5.39 us
    dot_general x1, matrix products, on_device(): jnp.dot(flat, whole_basis, preferred_element_type=jnp.float32)  2.87 us
  transfers between devices with their start and end apart: 10, of which 4 were waited for; matrix products, arithmetic and copies ran while one was open for 3% of the time, Pallas kernels for 0%

commit v1 on v0

--- a/solution.py
+++ b/solution.py
@@ -72,7 +72,22 @@
 def on_device(patterns, basis, valid, strength):
     cells_x, cells_y, pixels = patterns.shape
     flat = patterns.reshape(cells_x * cells_y, pixels)
-    whole_basis = lax.all_gather(basis, ("sx", "sy"), axis=1, tiled=True)
+    workers = lax.axis_size(("sx", "sy"))
+    column = tuple(((idx, (idx + 1) % workers) for idx in range(workers)))
+    right_arr, found_now = ([basis], [basis])
+    in_order = tuple(((idx, (idx - 1) % workers) for idx in range(workers)))
+    for _ in range(workers // 2):
+        current_block = lax.ppermute(right_arr[-1], ("sx", "sy"), column)
+        right_arr.append(current_block)
+    u = 0
+    while u < (workers - 1) // 2:
+        top = lax.ppermute(found_now[-1], ("sx", "sy"), in_order)
+        found_now.append(top)
+        u += 1
+    kept_arr = jnp.concatenate([*right_arr[::-1], *found_now[1:]], 1)
+    whole_basis = jnp.roll(
+        kept_arr, shift=(lax.axis_index(("sx", "sy")) - workers // 2) * basis.shape[1], axis=1
+    )
     partial_value = jnp.dot(flat, whole_basis, preferred_element_type=jnp.float32)
     partial_value = partial_value.reshape(cells_x, cells_y, partial_value.shape[1])
     mask_full = valid.astype(jnp.float32)

time: 118 us -> 122 us (1.034)
  starting transfers between devices: 21.4 us -> 27.9 us
  waiting for transfers between devices: 64.1 us -> 60.4 us
  local copies, waits for them, and re-layouts: 2.33 us -> 5.85 us
  matrix products: 5.06 us -> 3 us
    all_gather x1 -> x0, waiting for transfers between devices: 28.3 us -> none  [on_device(): whole_basis = lax.all_gather(basis, ('sx', 'sy'), axis=1, tiled=True)]
    ppermute x0 -> x7, waiting for transfers between devices: none -> 22.3 us  [the longest x4 22 us: on_device(): current_block = lax.ppermute(right_arr[-1], ('sx', 'sy'), column)]
    ppermute x0 -> x7, starting transfers between devices: none -> 7.96 us  [the longest x3 5.89 us: on_device(): top = lax.ppermute(found_now[-1], ('sx', 'sy'), in_order)]
    psum x1, waiting for transfers between devices: 28.8 us -> 32.8 us  [on_device(): coeffs = lax.psum(partial_value, 'px')]
    ppermute x4, starting transfers between devices: 14.9 us -> 12.3 us  [extended(): before = lax.ppermute(last, axis, up)]
    unnamed x12 -> x31, local copies, waits for them, and re-layouts: 1.19 us -> 3.69 us
    dot_general x1, matrix products: 2.87 us -> 0.8 us  [on_device(): jnp.dot(flat, whole_basis, preferred_element_type=jnp.float32)]
    ppermute x4, waiting for transfers between devices: 6.18 us -> 4.41 us  [extended(): after = lax.ppermute(initial, axis, down)]
  transfers between devices with their start and end apart: 10 -> 16, of which waited for: 4 -> 10; matrix products, arithmetic and copies ran while one was open for 3% -> 4% of each run, Pallas kernels for 0% -> 0%
where the time goes in v1:
time: 122 us
  waiting for transfers between devices  60.4 us (50%)
  starting transfers between devices  27.9 us (23%)
  between operations  13.8 us (11%)
  other arithmetic  11.1 us (9%)
  local copies, waits for them, and re-layouts  5.85 us (5%)
  matrix products  3 us (2%)
    psum x1, waiting for transfers between devices, on_device(): coeffs = lax.psum(partial_value, 'px')  32.8 us
    ppermute x4, waiting for transfers between devices, on_device(): current_block = lax.ppermute(right_arr[-1], ('sx', 'sy'), column)  22 us
    ppermute x4, starting transfers between devices, extended(): before = lax.ppermute(last, axis, up)  12.3 us
    ppermute x4, starting transfers between devices, extended(): after = lax.ppermute(initial, axis, down)  7.6 us
    ppermute x3, starting transfers between devices, on_device(): top = lax.ppermute(found_now[-1], ('sx', 'sy'), in_order)  5.89 us
    convert_element_type x1, other arithmetic, on_device(): blend(coeffs, padded, mask_pad, gaps, strength).astype(jnp.bfloat16)  5.44 us
    reduce_sum x5, other arithmetic, squared_gaps(): gaps.append(jnp.sum(differ * differ, axis=-1))  5.38 us
    ppermute x4, waiting for transfers between devices, extended(): after = lax.ppermute(initial, axis, down)  4.41 us
  transfers between devices with their start and end apart: 16, of which 10 were waited for; matrix products, arithmetic and copies ran while one was open for 4% of the time, Pallas kernels for 0%

profile of v1, /device:TPU:1, one launch (start us, length us, event | category | flops | bytes accessed | tf_op | source)
XLA Modules:
  0.0 122.0 jit_solution(3688364553190930410)
XLA Ops:
  6.5 2.1 %collective-permute-start = (bf16[2304,32]{0,1:T(8,128)(2,1)}, bf16[2304,32]{0,1:T(8,128)(2,1)S(1)}, u32[]{:S(2)}, u32[]{:S(2)}) collective-permute-start(bf16[2304,32]{0,1:T(8,128)(2,1)} %param.5), channel_id=1, source_target_pairs={{0,4},{4,8},{8,12},{12,16},{16,20},{20,24},{24,28},{28,0},{1,5},{5... | collective-permute-start | bytes 442376 | tf_op jit(solution)/shard_map/ppermute | solution.py:80
  8.6 5.2 %collective-permute-done = bf16[2304,32]{0,1:T(8,128)(2,1)S(1)} collective-permute-done((bf16[2304,32]{0,1:T(8,128)(2,1)}, bf16[2304,32]{0,1:T(8,128)(2,1)S(1)}, u32[]{:S(2)}, u32[]{:S(2)}) %collective-permute-start) | collective-permute-done | bytes 147488 | tf_op jit(solution)/shard_map/ppermute | solution.py:80
  13.8 0.0 collective-permute-start.1
  13.8 1.7 %collective-permute-start.4 = (bf16[2304,32]{0,1:T(8,128)(2,1)}, bf16[2304,32]{0,1:T(8,128)(2,1)S(1)}, u32[]{:S(2)}, u32[]{:S(2)}) collective-permute-start(bf16[2304,32]{0,1:T(8,128)(2,1)} %param.5), channel_id=1, source_target_pairs={{0,28},{4,0},{8,4},{12,8},{16,12},{20,16},{24,20},{28,24},{1,29},{... | collective-permute-start | bytes 442376 | tf_op jit(solution)/shard_map/ppermute | solution.py:84
  15.6 5.4 %collective-permute-done.1 = bf16[2304,32]{0,1:T(8,128)(2,1)S(1)} collective-permute-done((bf16[2304,32]{0,1:T(8,128)(2,1)S(1)}, bf16[2304,32]{0,1:T(8,128)(2,1)S(1)}, u32[]{:S(2)}, u32[]{:S(2)}) %collective-permute-start.1) | collective-permute-done | bytes 147488 | tf_op jit(solution)/shard_map/ppermute | solution.py:80
  21.0 0.0 collective-permute-start.2
  21.0 0.4 collective-permute-done.4
  21.4 1.9 %collective-permute-start.5 = (bf16[2304,32]{0,1:T(8,128)(2,1)S(1)}, bf16[2304,32]{0,1:T(8,128)(2,1)S(1)}, u32[]{:S(2)}, u32[]{:S(2)}) collective-permute-start(bf16[2304,32]{0,1:T(8,128)(2,1)S(1)} %collective-permute-done.4), channel_id=1, source_target_pairs={{0,28},{4,0},{8,4},{12,8},{16,12},{20,16},{24,20},{28,24},{1,29},{... | collective-permute-start | bytes 442376 | tf_op jit(solution)/shard_map/ppermute | solution.py:84
  23.3 5.5 %collective-permute-done.2 = bf16[2304,32]{0,1:T(8,128)(2,1)S(1)} collective-permute-done((bf16[2304,32]{0,1:T(8,128)(2,1)S(1)}, bf16[2304,32]{0,1:T(8,128)(2,1)S(1)}, u32[]{:S(2)}, u32[]{:S(2)}) %collective-permute-start.2) | collective-permute-done | bytes 147488 | tf_op jit(solution)/shard_map/ppermute | solution.py:80
  28.7 0.0 collective-permute-start.3
  28.7 0.0 collective-permute-done.5
  28.7 2.3 %collective-permute-start.6 = (bf16[2304,32]{0,1:T(8,128)(2,1)S(1)}, bf16[2304,32]{0,1:T(8,128)(2,1)S(1)}, u32[]{:S(2)}, u32[]{:S(2)}) collective-permute-start(bf16[2304,32]{0,1:T(8,128)(2,1)S(1)} %collective-permute-done.5), channel_id=1, source_target_pairs={{0,28},{4,0},{8,4},{12,8},{16,12},{20,16},{24,20},{28,24},{1,29},{... | collective-permute-start | bytes 442376 | tf_op jit(solution)/shard_map/ppermute | solution.py:84
  31.0 5.8 %collective-permute-done.3 = bf16[2304,32]{0,1:T(8,128)(2,1)S(1)} collective-permute-done((bf16[2304,32]{0,1:T(8,128)(2,1)S(1)}, bf16[2304,32]{0,1:T(8,128)(2,1)S(1)}, u32[]{:S(2)}, u32[]{:S(2)}) %collective-permute-start.3) | collective-permute-done | bytes 147488 | tf_op jit(solution)/shard_map/ppermute | solution.py:80
  36.9 0.9 constant_dynamic-update-slice_fusion.11
  38.1 0.0 copy-start.2
  38.1 1.4 %copy-done.2 = bf16[2304,512]{0,1:T(8,128)(2,1)} copy-done((bf16[2304,512]{0,1:T(8,128)(2,1)}, bf16[2304,512]{0,1:T(8,128)(2,1)S(1)}, u32[]{:S(2)}) %copy-start.2) | copy-done | bytes 2359320
  39.5 0.8 convolution_bitcast_fusion
  40.3 1.0 copy.5
  41.3 0.0 all-reduce.2.cloned.1.call-update
  41.4 3.1 %collective-permute-start.8 = (f32[3,32]{1,0:T(4,128)S(1)}, f32[3,32]{1,0:T(4,128)S(1)}, u32[]{:S(2)}, u32[]{:S(2)}) collective-permute-start(f32[3,32]{1,0:T(4,128)S(1)} %get-tuple-element.125), channel_id=1, source_target_pairs={{8,0},{16,8},{24,16},{9,1},{17,9},{25,17},{10,2},{18,10},{26,18},{... | collective-permute-start | bytes 1160 | tf_op jit(solution)/shard_map/ppermute | solution.py:18
  44.5 2.4 %collective-permute-start.7 = (f32[3,32]{1,0:T(4,128)S(1)}, f32[3,32]{1,0:T(4,128)S(1)}, u32[]{:S(2)}, u32[]{:S(2)}) collective-permute-start(f32[3,32]{1,0:T(4,128)S(1)} %get-tuple-element.124), channel_id=1, source_target_pairs={{0,8},{8,16},{16,24},{1,9},{9,17},{17,25},{2,10},{10,18},{18,26},{... | collective-permute-start | bytes 1160 | tf_op jit(solution)/shard_map/ppermute | solution.py:17
  47.0 0.7 collective-permute-done.7
  47.7 32.8 %all-reduce.2.cloned.1.call-done = f32[16,32,256]{2,1,0:T(8,128)} async-done(((f32[16,32,256]{2,1,0:T(8,128)}), f32[16,32,256]{2,1,0:T(8,128)}) %all-reduce.2.cloned.1.call-update) | async-done | bytes 524304 | tf_op jit(solution)/shard_map/psum | solution.py:94
  80.5 1.0 fusion.61
  81.5 4.6 %collective-permute-start.10 = (f32[3,32,256]{2,1,0:T(8,128)S(1)}, f32[3,32,256]{2,1,0:T(8,128)S(1)}, u32[]{:S(2)}, u32[]{:S(2)}) collective-permute-start(f32[3,32,256]{2,1,0:T(8,128)S(1)} %get-tuple-element.116), channel_id=1, source_target_pairs={{0,8},{8,16},{16,24},{1,9},{9,17},{17,25},{2,10},{10,18},{18,26},{... | collective-permute-start | bytes 294920 | tf_op jit(solution)/shard_map/ppermute | solution.py:17
  86.1 0.1 fusion.62
  86.1 1.3 %collective-permute-start.13 = (f32[22,3]{1,0:T(8,128)S(1)}, f32[22,3]{1,0:T(8,128)S(1)}, u32[]{:S(2)}, u32[]{:S(2)}) collective-permute-start(f32[22,3]{1,0:T(8,128)S(1)} %get-tuple-element.122), channel_id=1, source_target_pairs={{4,0},{5,1},{6,2},{7,3},{12,8},{13,9},{14,10},{15,11},{20,16},{21,... | collective-permute-start | bytes 800 | tf_op jit(solution)/shard_map/ppermute | solution.py:18
  87.4 4.0 %collective-permute-start.9 = (f32[22,3]{1,0:T(8,128)S(1)}, f32[22,3]{1,0:T(8,128)S(1)}, u32[]{:S(2)}, u32[]{:S(2)}) collective-permute-start(f32[22,3]{1,0:T(8,128)S(1)} %get-tuple-element.123), channel_id=1, source_target_pairs={{0,4},{1,5},{2,6},{3,7},{8,12},{9,13},{10,14},{11,15},{16,20},{17,... | collective-permute-start | bytes 800 | tf_op jit(solution)/shard_map/ppermute | solution.py:17
  91.4 1.9 %collective-permute-start.11 = (f32[3,32,256]{2,1,0:T(8,128)S(1)}, f32[3,32,256]{2,1,0:T(8,128)S(1)}, u32[]{:S(2)}, u32[]{:S(2)}) collective-permute-start(f32[3,32,256]{2,1,0:T(8,128)S(1)} %get-tuple-element.117), channel_id=1, source_target_pairs={{8,0},{16,8},{24,16},{9,1},{17,9},{25,17},{10,2},{18,10},{26,18},{... | collective-permute-start | bytes 294920 | tf_op jit(solution)/shard_map/ppermute | solution.py:18
  93.3 0.0 collective-permute-done.10
  93.4 1.2 constant_dynamic-update-slice_fusion.17
  94.5 2.8 %collective-permute-done.11 = f32[3,32,256]{2,1,0:T(8,128)S(1)} collective-permute-done((f32[3,32,256]{2,1,0:T(8,128)S(1)}, f32[3,32,256]{2,1,0:T(8,128)S(1)}, u32[]{:S(2)}, u32[]{:S(2)}) %collective-permute-start.11) | collective-permute-done | bytes 98336 | tf_op jit(solution)/shard_map/ppermute | solution.py:18
  97.4 1.3 %collective-permute-start.12 = (f32[22,3,256]{2,1,0:T(4,128)S(1)}, f32[22,3,256]{2,1,0:T(4,128)S(1)}, u32[]{:S(2)}, u32[]{:S(2)}) collective-permute-start(f32[22,3,256]{2,1,0:T(4,128)S(1)} %get-tuple-element.112), channel_id=1, source_target_pairs={{0,4},{1,5},{2,6},{3,7},{8,12},{9,13},{10,14},{11,15},{16,20},{17,... | collective-permute-start | bytes 202760 | tf_op jit(solution)/shard_map/ppermute | solution.py:17
  98.7 0.0 collective-permute-done.13
  98.7 0.1 pad_maximum_fusion.3
  98.8 1.3 %collective-permute-start.14 = (f32[22,3,256]{2,1,0:T(4,128)S(1)}, f32[22,3,256]{2,1,0:T(4,128)S(1)}, u32[]{:S(2)}, u32[]{:S(2)}) collective-permute-start(f32[22,3,256]{2,1,0:T(4,128)S(1)} %get-tuple-element.111), channel_id=1, source_target_pairs={{4,0},{5,1},{6,2},{7,3},{12,8},{13,9},{14,10},{15,11},{20,16},{21,... | collective-permute-start | bytes 202760 | tf_op jit(solution)/shard_map/ppermute | solution.py:18
  100.1 0.1 collective-permute-done.12
  100.2 1.1 multiply_reduce_fusion.46
  101.4 1.1 multiply_reduce_fusion.47
  102.5 1.6 %collective-permute-done.14 = f32[22,3,256]{2,1,0:T(4,128)S(1)} collective-permute-done((f32[22,3,256]{2,1,0:T(4,128)S(1)}, f32[22,3,256]{2,1,0:T(4,128)S(1)}, u32[]{:S(2)}, u32[]{:S(2)}) %collective-permute-start.14) | collective-permute-done | bytes 67616 | tf_op jit(solution)/shard_map/ppermute | solution.py:18
  104.1 1.0 multiply_reduce_fusion.42
  105.1 1.0 multiply_reduce_fusion.43
  106.1 0.0 copy-start.5
  106.1 1.2 multiply_reduce_fusion.45
  107.3 0.2 add_add_fusion
  107.5 0.0 copy-start.3
  107.5 5.4 %divide_convert_fusion = bf16[16,32,256]{2,1,0:T(8,128)(2,1)S(1)} fusion(f32[16,32,256]{2,1,0:T(8,128)S(1)} %copy-done.1, f32[19,32,256]{2,1,0:T(8,128)S(1)} %constant_dynamic-update-slice_fusion.21, f32[19,32,256]{2,1,0:T(8,128)S(1)} %get-tuple-element.115, f32[22,32,256]{2,1,0:T(8,128)S(1)} %constant_dynamic-update-slice_fusion.16, ...), kind=kLoop, calls=%fused_computation.126 | loop fusion | flops 18350080 | bytes 4888576 | tf_op jit(solution)/shard_map/convert_element_type | solution.py:97
  113.0 2.2 %convolution_convert_fusion = bf16[512,2304]{1,0:T(8,128)(2,1)} fusion(bf16[512,256]{1,0:T(8,128)(2,1)S(1)} %bitcast.10, bf16[2304,512]{0,1:T(8,128)(2,1)S(1)} %copy-done.3, s32[]{:T(128)S(6)} %select_n.14), kind=kOutput, calls=%fused_computation.40 | convolution fusion | flops 605159424 | bytes 3801092 | tf_op jit(solution)/shard_map/dot_general | solution.py:99
  (36 shorter events, 0.3 us)
Async XLA Ops:
  6.5 31.6 %copy-start = (bf16[16,32,2304]{2,1,0:T(8,128)(2,1)S(1)}, bf16[16,32,2304]{2,1,0:T(8,128)(2,1)}, u32[]{:S(2)}) copy-start(bf16[16,32,2304]{2,1,0:T(8,128)(2,1)} %param.4) | copy-start | bytes 7077892
  6.5 31.5 %copy-start.4 = (bf16[2304,32]{0,1:T(8,128)(2,1)S(1)}, bf16[2304,32]{0,1:T(8,128)(2,1)}, u32[]{:S(2)}) copy-start(bf16[2304,32]{0,1:T(8,128)(2,1)} %param.5) | copy-start | bytes 442372
  6.5 73.9 %all-reduce.2.cloned.1.call-start = ((), (), s32[]{:S(2)}) async-start(), calls=%async_computation | async-start | bytes 1048576 | tf_op jit(solution)/shard_map/psum | solution.py:94
  6.5 7.3 %collective-permute-start = (bf16[2304,32]{0,1:T(8,128)(2,1)}, bf16[2304,32]{0,1:T(8,128)(2,1)S(1)}, u32[]{:S(2)}, u32[]{:S(2)}) collective-permute-start(bf16[2304,32]{0,1:T(8,128)(2,1)} %param.5), channel_id=1, source_target_pairs={{0,4},{4,8},{8,12},{12,16},{16,20},{20,24},{24,28},{28,0},{1,5},{5... | collective-permute-start | bytes 442376 | tf_op jit(solution)/shard_map/ppermute | solution.py:80
  13.8 7.2 %collective-permute-start.1 = (bf16[2304,32]{0,1:T(8,128)(2,1)S(1)}, bf16[2304,32]{0,1:T(8,128)(2,1)S(1)}, u32[]{:S(2)}, u32[]{:S(2)}) collective-permute-start(bf16[2304,32]{0,1:T(8,128)(2,1)S(1)} %collective-permute-done), channel_id=1, source_target_pairs={{0,4},{4,8},{8,12},{12,16},{16,20},{20,24},{24,28},{28,0},{1,5},{5... | collective-permute-start | bytes 442376 | tf_op jit(solution)/shard_map/ppermute | solution.py:80
  13.8 7.6 %collective-permute-start.4 = (bf16[2304,32]{0,1:T(8,128)(2,1)}, bf16[2304,32]{0,1:T(8,128)(2,1)S(1)}, u32[]{:S(2)}, u32[]{:S(2)}) collective-permute-start(bf16[2304,32]{0,1:T(8,128)(2,1)} %param.5), channel_id=1, source_target_pairs={{0,28},{4,0},{8,4},{12,8},{16,12},{20,16},{24,20},{28,24},{1,29},{... | collective-permute-start | bytes 442376 | tf_op jit(solution)/shard_map/ppermute | solution.py:84
  21.0 7.8 %collective-permute-start.2 = (bf16[2304,32]{0,1:T(8,128)(2,1)S(1)}, bf16[2304,32]{0,1:T(8,128)(2,1)S(1)}, u32[]{:S(2)}, u32[]{:S(2)}) collective-permute-start(bf16[2304,32]{0,1:T(8,128)(2,1)S(1)} %collective-permute-done.1), channel_id=1, source_target_pairs={{0,4},{4,8},{8,12},{12,16},{16,20},{20,24},{24,28},{28,0},{1,5},{5... | collective-permute-start | bytes 442376 | tf_op jit(solution)/shard_map/ppermute | solution.py:80
  21.4 7.4 %collective-permute-start.5 = (bf16[2304,32]{0,1:T(8,128)(2,1)S(1)}, bf16[2304,32]{0,1:T(8,128)(2,1)S(1)}, u32[]{:S(2)}, u32[]{:S(2)}) collective-permute-start(bf16[2304,32]{0,1:T(8,128)(2,1)S(1)} %collective-permute-done.4), channel_id=1, source_target_pairs={{0,28},{4,0},{8,4},{12,8},{16,12},{20,16},{24,20},{28,24},{1,29},{... | collective-permute-start | bytes 442376 | tf_op jit(solution)/shard_map/ppermute | solution.py:84
  28.7 8.1 %collective-permute-start.3 = (bf16[2304,32]{0,1:T(8,128)(2,1)S(1)}, bf16[2304,32]{0,1:T(8,128)(2,1)S(1)}, u32[]{:S(2)}, u32[]{:S(2)}) collective-permute-start(bf16[2304,32]{0,1:T(8,128)(2,1)S(1)} %collective-permute-done.2), channel_id=1, source_target_pairs={{0,4},{4,8},{8,12},{12,16},{16,20},{20,24},{24,28},{28,0},{1,5},{5... | collective-permute-start | bytes 442376 | tf_op jit(solution)/shard_map/ppermute | solution.py:80
  28.7 9.1 %collective-permute-start.6 = (bf16[2304,32]{0,1:T(8,128)(2,1)S(1)}, bf16[2304,32]{0,1:T(8,128)(2,1)S(1)}, u32[]{:S(2)}, u32[]{:S(2)}) collective-permute-start(bf16[2304,32]{0,1:T(8,128)(2,1)S(1)} %collective-permute-done.5), channel_id=1, source_target_pairs={{0,28},{4,0},{8,4},{12,8},{16,12},{20,16},{24,20},{28,24},{1,29},{... | collective-permute-start | bytes 442376 | tf_op jit(solution)/shard_map/ppermute | solution.py:84
  38.1 1.4 %copy-start.2 = (bf16[2304,512]{0,1:T(8,128)(2,1)}, bf16[2304,512]{0,1:T(8,128)(2,1)S(1)}, u32[]{:S(2)}) copy-start(bf16[2304,512]{0,1:T(8,128)(2,1)S(1)} %constant_dynamic-update-slice_fusion) | copy-start | bytes 7077892
  39.5 1.9 %copy-start.6 = (s32[16,32]{1,0:T(8,128)S(1)}, s32[16,32]{1,0:T(8,128)}, u32[]{:S(2)}) copy-start(s32[16,32]{1,0:T(8,128)} %param.6) | copy-start | bytes 6148
  41.4 5.6 %collective-permute-start.8 = (f32[3,32]{1,0:T(4,128)S(1)}, f32[3,32]{1,0:T(4,128)S(1)}, u32[]{:S(2)}, u32[]{:S(2)}) collective-permute-start(f32[3,32]{1,0:T(4,128)S(1)} %get-tuple-element.125), channel_id=1, source_target_pairs={{8,0},{16,8},{24,16},{9,1},{17,9},{25,17},{10,2},{18,10},{26,18},{... | collective-permute-start | bytes 1160 | tf_op jit(solution)/shard_map/ppermute | solution.py:18
  44.5 3.2 %collective-permute-start.7 = (f32[3,32]{1,0:T(4,128)S(1)}, f32[3,32]{1,0:T(4,128)S(1)}, u32[]{:S(2)}, u32[]{:S(2)}) collective-permute-start(f32[3,32]{1,0:T(4,128)S(1)} %get-tuple-element.124), channel_id=1, source_target_pairs={{0,8},{8,16},{16,24},{1,9},{9,17},{17,25},{2,10},{10,18},{18,26},{... | collective-permute-start | bytes 1160 | tf_op jit(solution)/shard_map/ppermute | solution.py:17
  80.5 19.8 %copy-start.1 = (f32[16,32,256]{2,1,0:T(8,128)S(1)}, f32[16,32,256]{2,1,0:T(8,128)}, u32[]{:S(2)}) copy-start(f32[16,32,256]{2,1,0:T(8,128)} %all-reduce.2.cloned.1.call-done) | copy-start | bytes 1572868
  81.5 11.9 %collective-permute-start.10 = (f32[3,32,256]{2,1,0:T(8,128)S(1)}, f32[3,32,256]{2,1,0:T(8,128)S(1)}, u32[]{:S(2)}, u32[]{:S(2)}) collective-permute-start(f32[3,32,256]{2,1,0:T(8,128)S(1)} %get-tuple-element.116), channel_id=1, source_target_pairs={{0,8},{8,16},{16,24},{1,9},{9,17},{17,25},{2,10},{10,18},{18,26},{... | collective-permute-start | bytes 294920 | tf_op jit(solution)/shard_map/ppermute | solution.py:17
  86.1 12.6 %collective-permute-start.13 = (f32[22,3]{1,0:T(8,128)S(1)}, f32[22,3]{1,0:T(8,128)S(1)}, u32[]{:S(2)}, u32[]{:S(2)}) collective-permute-start(f32[22,3]{1,0:T(8,128)S(1)} %get-tuple-element.122), channel_id=1, source_target_pairs={{4,0},{5,1},{6,2},{7,3},{12,8},{13,9},{14,10},{15,11},{20,16},{21,... | collective-permute-start | bytes 800 | tf_op jit(solution)/shard_map/ppermute | solution.py:18
  87.4 11.3 %collective-permute-start.9 = (f32[22,3]{1,0:T(8,128)S(1)}, f32[22,3]{1,0:T(8,128)S(1)}, u32[]{:S(2)}, u32[]{:S(2)}) collective-permute-start(f32[22,3]{1,0:T(8,128)S(1)} %get-tuple-element.123), channel_id=1, source_target_pairs={{0,4},{1,5},{2,6},{3,7},{8,12},{9,13},{10,14},{11,15},{16,20},{17,... | collective-permute-start | bytes 800 | tf_op jit(solution)/shard_map/ppermute | solution.py:17
  91.4 5.9 %collective-permute-start.11 = (f32[3,32,256]{2,1,0:T(8,128)S(1)}, f32[3,32,256]{2,1,0:T(8,128)S(1)}, u32[]{:S(2)}, u32[]{:S(2)}) collective-permute-start(f32[3,32,256]{2,1,0:T(8,128)S(1)} %get-tuple-element.117), channel_id=1, source_target_pairs={{8,0},{16,8},{24,16},{9,1},{17,9},{25,17},{10,2},{18,10},{26,18},{... | collective-permute-start | bytes 294920 | tf_op jit(solution)/shard_map/ppermute | solution.py:18
  97.4 2.8 %collective-permute-start.12 = (f32[22,3,256]{2,1,0:T(4,128)S(1)}, f32[22,3,256]{2,1,0:T(4,128)S(1)}, u32[]{:S(2)}, u32[]{:S(2)}) collective-permute-start(f32[22,3,256]{2,1,0:T(4,128)S(1)} %get-tuple-element.112), channel_id=1, source_target_pairs={{0,4},{1,5},{2,6},{3,7},{8,12},{9,13},{10,14},{11,15},{16,20},{17,... | collective-permute-start | bytes 202760 | tf_op jit(solution)/shard_map/ppermute | solution.py:17
  98.8 5.3 %collective-permute-start.14 = (f32[22,3,256]{2,1,0:T(4,128)S(1)}, f32[22,3,256]{2,1,0:T(4,128)S(1)}, u32[]{:S(2)}, u32[]{:S(2)}) collective-permute-start(f32[22,3,256]{2,1,0:T(4,128)S(1)} %get-tuple-element.111), channel_id=1, source_target_pairs={{4,0},{5,1},{6,2},{7,3},{12,8},{13,9},{14,10},{15,11},{20,16},{21,... | collective-permute-start | bytes 202760 | tf_op jit(solution)/shard_map/ppermute | solution.py:18
  106.1 1.2 copy-start.5
  107.5 5.5 %copy-start.3 = (bf16[2304,512]{0,1:T(8,128)(2,1)S(1)}, bf16[2304,512]{0,1:T(8,128)(2,1)}, u32[]{:S(2)}) copy-start(bf16[2304,512]{0,1:T(8,128)(2,1)} %copy-done.2) | copy-start | bytes 7077892
Sparse Core Ops, SparseCore 0:
  41.5 38.9 all-reduce.1
